TPU v7x, 32 devices: a whole 2x2x4 slice. The times are simulated.
32 devices in a mesh: vocab: 4 (over y, x), dp: 8 (over z, core).
Axes of the slice: x: 2, y: 2, z: 4, core: 2. Of those that a mesh axis runs over, the one named last changes fastest.
Arguments:
- grads: bfloat16 [4096, 4096], P(('vocab', 'dp')), may hold values from -6 to 6
- token_ids: int32 [4096], P(('vocab', 'dp')), may hold values from 0 to 32063, as said below
Outputs:
- grad_table: float32 [32064, 4096], P('vocab', 'dp')
- row_share: float32 [32064], P('vocab')
Inputs may be any that keep to these rules, and one draw needn't show every extreme that they name: `token_ids`: within the 128 ids of one device (aligned blocks in order) the ids never fall; at most 32 of them lie in the rows k * 8016 to (k + 1) * 8016 - 1 of any one k, and in every block some k has exactly 32.
All inputs are finite; a program needn't handle non-finite values.
Results may differ from a plain program's by a relative error of at most 0.0003.
Values may be sent and summed in bfloat16 or wider, within the bound.
No kernel may reach another device: no remote copies, remote signals or barrier semaphores. Data moves between devices by JAX's collectives and lax.ppermute only.
A program may use at most 64 MiB of HBM per device.

v0:
```python
import math
import jax
import jax.numpy as jnp
from jax import lax
from jax.sharding import PartitionSpec as P

VOCAB_DEV = 8016
TOK_DEV = 128
CAP = 32


def bucket(id_blocks, data_blocks, n_vocab):
    owner_start = jnp.arange(n_vocab, dtype=jnp.int32) * VOCAB_DEV
    starts = jnp.sum((id_blocks[:, None, :] < owner_start[None, :, None]).astype(jnp.int32), axis=2)
    length = id_blocks.shape[1]
    finish = jnp.concatenate(
        [starts[:, 1:], jnp.full((starts.shape[0], 1), length, jnp.int32)], axis=1
    )
    amount = jnp.transpose(finish - starts, (1, 0))
    begins = jnp.transpose(starts, (1, 0))
    slot = jnp.arange(CAP, dtype=jnp.int32)
    places = begins[:, :, None] + slot[None, None, :]
    valid = slot[None, None, :] < amount[:, :, None]
    columns = jnp.arange(length, dtype=jnp.int32)
    select = (places[:, :, :, None] == columns[None, None, None, :]) & valid[:, :, :, None]
    rows = jnp.einsum(
        "vbcl,bld->vbcd",
        select.astype(data_blocks.dtype),
        data_blocks,
        preferred_element_type=jnp.float32,
    )
    rows = rows.astype(data_blocks.dtype).reshape(-1, data_blocks.shape[2])
    picked = jnp.sum(jnp.where(select, id_blocks[None, :, None, :], 0), axis=3)
    slot_ids = jnp.where(valid, picked, -1).reshape(-1)
    return (rows, slot_ids)


def local(grads, token_ids):
    n_vocab = lax.axis_size("vocab")
    n_data = lax.axis_size("dp")
    spread_ids = jnp.broadcast_to(token_ids[:, None], (token_ids.shape[0], n_data))
    split_rows, split_ids = (
        lax.all_to_all(grads, "dp", split_axis=1, concat_axis=0, tiled=True),
        lax.all_to_all(spread_ids, "dp", split_axis=1, concat_axis=0, tiled=True),
    )
    group_ids = split_ids.reshape(n_data, -1)
    group_rows = split_rows.reshape(n_data, group_ids.shape[1], split_rows.shape[1])
    rows, slot_ids = bucket(group_ids, group_rows, n_vocab)
    mine, mine_ids = (
        lax.all_to_all(rows, "vocab", split_axis=0, concat_axis=0, tiled=True),
        lax.all_to_all(slot_ids, "vocab", split_axis=0, concat_axis=0, tiled=True),
    )
    local_rows = jnp.where(mine_ids < 0, -1, mine_ids - lax.axis_index("vocab") * VOCAB_DEV)
    total = local_rows.shape[0]
    width = math.gcd(total, 512)
    row_blocks = mine.reshape(total // width, width, mine.shape[1])
    id_parts = local_rows.reshape(total // width, width)
    table_rows = jnp.arange(VOCAB_DEV, dtype=jnp.int32)

    def accumulate(carry, item):
        table, counts = carry
        block, ids = item
        onehot = ids[:, None] == table_rows[None, :]
        table = table + lax.dot_general(
            onehot.astype(block.dtype),
            block,
            (((0,), (0,)), ((), ())),
            preferred_element_type=jnp.float32,
        )
        counts = counts + jnp.sum(onehot.astype(jnp.float32), axis=0)
        return ((table, counts), None)

    start = (
        jnp.zeros((VOCAB_DEV, mine.shape[1]), jnp.float32),
        jnp.zeros((VOCAB_DEV,), jnp.float32),
    )
    (grad_table, counts), _ = lax.scan(accumulate, start, (row_blocks, id_parts))
    row_share = counts * (VOCAB_DEV / (TOK_DEV * n_data))
    return (grad_table, row_share)


def solution(mesh):
    in_specs = (P(("vocab", "dp"), None), P(("vocab", "dp")))
    out_specs = (P("vocab", "dp"), P("vocab"))
    return jax.shard_map(local, mesh=mesh, in_specs=in_specs, out_specs=out_specs, check_vma=False)
```

profile of v0, /device:TPU:0, one launch (start us, length us, event | category | flops | bytes accessed | tf_op | source)
XLA Modules:
  0.0 92.9 jit_solution(14292049239312270715)
XLA Ops:
  0.6 1.3 %broadcast_in_dim.26 = s32[128,8,1]{0,2,1:T(1,128)} broadcast(s32[128]{0:T(128)} %param.5), dimensions={0} | broadcast | bytes 4608 | tf_op jit(solution)/shard_map/broadcast_in_dim | solution.py:41
  1.9 6.4 %all-to-all-start = ((s32[128,8,1]{0,2,1:T(1,128)}), s32[128,8,1]{0,2,1:T(1,128)S(1)}, u32[]{:S(2)}, u32[]{:S(2)}) async-start(s32[128,8,1]{0,2,1:T(1,128)} %broadcast_in_dim.26), calls=%async_computation | async-start | bytes 8192 | tf_op jit(solution)/shard_map/all_to_all | solution.py:44
  8.2 1.6 %copy.29 = bf16[128,4096]{0,1:T(8,128)(2,1)S(1)} copy(bf16[128,4096]{1,0:T(8,128)(2,1)} %param.4) | data formatting | bytes 2097152 | tf_op args[0]
  9.9 1.3 %copy.30 = bf16[128,8,512]{2,0,1:T(8,128)(2,1)} copy(bf16[128,8,512]{0,2,1:T(8,128)(2,1)S(1)} %bitcast.29) | data formatting | bytes 2097152 | tf_op jit(solution)/shard_map/all_to_all | solution.py:43
  11.2 2.6 %all-to-all-done = s32[128,8,1]{0,2,1:T(1,128)S(1)} async-done(((s32[128,8,1]{0,2,1:T(1,128)}), s32[128,8,1]{0,2,1:T(1,128)S(1)}, u32[]{:S(2)}, u32[]{:S(2)}) %all-to-all-start) | async-done | bytes 4128 | tf_op jit(solution)/shard_map/all_to_all | solution.py:44
  13.7 3.6 %all-to-all-start.2 = ((bf16[128,8,512]{2,0,1:T(8,128)(2,1)}), bf16[128,8,512]{2,0,1:T(8,128)(2,1)S(1)}, u32[]{:S(2)}, u32[]{:S(2)}) async-start(bf16[128,8,512]{2,0,1:T(8,128)(2,1)} %copy.30), calls=%async_computation.2 | async-start | bytes 2097152 | tf_op jit(solution)/shard_map/all_to_all | solution.py:43
  17.3 0.1 add.37
  17.4 0.2 convert_reduce_fusion
  17.6 0.1 iota_compare_fusion.5
  17.7 0.1 copy.23
  17.8 0.1 iota_add_fusion
  17.9 0.9 select_reduce_fusion
  18.8 0.1 reduce_sum.31
  18.9 0.1 lt.57
  19.0 0.1 lt.58
  19.1 0.6 copy.26
  19.7 24.1 %all-to-all-done.2 = bf16[128,8,512]{2,0,1:T(8,128)(2,1)S(1)} async-done(((bf16[128,8,512]{2,0,1:T(8,128)(2,1)}), bf16[128,8,512]{2,0,1:T(8,128)(2,1)S(1)}, u32[]{:S(2)}, u32[]{:S(2)}) %all-to-all-start.2) | async-done | bytes 1048608 | tf_op jit(solution)/shard_map/all_to_all | solution.py:43
  43.8 3.7 %all-to-all-start.1 = ((s32[4,256,1]{1,2,0:T(1,128)}), s32[4,256,1]{1,2,0:T(1,128)S(1)}, u32[]{:S(2)}, u32[]{:S(2)}) async-start(s32[4,256,1]{1,2,0:T(1,128)} %copy.26), calls=%async_computation.1 | async-start | bytes 8192 | tf_op jit(solution)/shard_map/all_to_all | solution.py:51
  47.5 0.5 fusion.9
  48.0 1.1 %copy.31 = bf16[4,8,32,512]{3,2,1,0:T(8,128)(2,1)} copy(bf16[4,8,32,512]{3,2,0,1:T(8,128)(2,1)S(1)} %fusion.9) | data formatting | bytes 2097152 | tf_op jit(solution)/shard_map/convert_element_type | solution.py:32
  49.1 3.1 %all-to-all-done.1 = s32[4,256,1]{1,2,0:T(1,128)S(1)} async-done(((s32[4,256,1]{1,2,0:T(1,128)}), s32[4,256,1]{1,2,0:T(1,128)S(1)}, u32[]{:S(2)}, u32[]{:S(2)}) %all-to-all-start.1) | async-done | bytes 4128 | tf_op jit(solution)/shard_map/all_to_all | solution.py:51
  52.2 3.5 %all-to-all-start.3 = ((bf16[4,256,512]{2,1,0:T(8,128)(2,1)}), bf16[4,256,512]{2,1,0:T(8,128)(2,1)S(1)}, u32[]{:S(2)}, u32[]{:S(2)}) async-start(bf16[4,256,512]{2,1,0:T(8,128)(2,1)} %bitcast.10), calls=%async_computation.3 | async-start | bytes 2097152 | tf_op jit(solution)/shard_map/all_to_all | solution.py:50
  55.8 12.1 %all-to-all-done.3 = bf16[4,256,512]{2,1,0:T(8,128)(2,1)S(1)} async-done(((bf16[4,256,512]{2,1,0:T(8,128)(2,1)}), bf16[4,256,512]{2,1,0:T(8,128)(2,1)S(1)}, u32[]{:S(2)}, u32[]{:S(2)}) %all-to-all-start.3) | async-done | bytes 1048608 | tf_op jit(solution)/shard_map/all_to_all | solution.py:50
  67.9 24.4 %while.13 = (s32[]{:T(128)}, f32[8016,512]{1,0:T(8,128)}, f32[8016]{0:T(1024)S(1)}, s32[2,512]{1,0:T(2,128)S(1)}, bf16[2,512,512]{2,1,0:T(8,128)(2,1)S(1)}, /*index=5*/s32[]{:T(128)}, s32[]{:T(128)}) while((s32[]{:T(128)}, f32[8016,512]{1,0:T(8,128)}, f32[8016]{0:T(1024)S(1)}, s32[2,512]{1,0:T(2,128)S(1)}, ...), condition=%wide.region_4.5_spmd.clone, body=%wide.region_2.4_spmd.clone.sunk | while | flops 4227325952 | bytes 33494372 | solution.py:77
  67.9 1.8 %fusion.18 = f32[8016]{0:T(1024)S(1)} fusion(s32[512]{0:T(512)S(1)} %bitcast.30), kind=kLoop, calls=%fused_computation.4.clone.1 | loop fusion | flops 12304560 | bytes 34112 | tf_op jit(solution)/shard_map/while/body/eval_jaxpr/reduce_sum | solution.py:70
  69.7 8.7 %select_add_fusion.4 = f32[8016,512]{1,0:T(8,128)} fusion(f32[8016,512]{1,0:T(8,128)} %get-tuple-element.106, s32[512]{0:T(512)S(1)} %bitcast.31, pred[]{:T(512)S(6)} %compare.4, bf16[2,512,512]{2,1,0:T(8,128)(2,1)S(1)} %get-tuple-element.116, s32[]{:T(128)S(6)} %copy.37), kind=kOutput, calls=%fused_computation.5.clone.1 | convolution fusion | flops 4215005184 | bytes 33359876 | tf_op jit(solution)/shard_map/while/body/eval_jaxpr/dot_general | solution.py:64
  78.4 1.8 %fusion.18 = f32[8016]{0:T(1024)S(1)} fusion(s32[512]{0:T(512)S(1)} %bitcast.30), kind=kLoop, calls=%fused_computation.4.clone.1 | loop fusion | flops 12304560 | bytes 34112 | tf_op jit(solution)/shard_map/while/body/eval_jaxpr/reduce_sum | solution.py:70
  80.3 12.0 %select_add_fusion.4 = f32[8016,512]{1,0:T(8,128)} fusion(f32[8016,512]{1,0:T(8,128)} %get-tuple-element.106, s32[512]{0:T(512)S(1)} %bitcast.31, pred[]{:T(512)S(6)} %compare.4, bf16[2,512,512]{2,1,0:T(8,128)(2,1)S(1)} %get-tuple-element.116, s32[]{:T(128)S(6)} %copy.37), kind=kOutput, calls=%fused_computation.5.clone.1 | convolution fusion | flops 4215005184 | bytes 33359876 | tf_op jit(solution)/shard_map/while/body/eval_jaxpr/dot_general | solution.py:64
  92.3 0.6 broadcast_multiply_fusion
  (15 shorter events, 0.1 us)
Async XLA Ops:
  1.9 11.9 %all-to-all-start = ((s32[128,8,1]{0,2,1:T(1,128)}), s32[128,8,1]{0,2,1:T(1,128)S(1)}, u32[]{:S(2)}, u32[]{:S(2)}) async-start(s32[128,8,1]{0,2,1:T(1,128)} %broadcast_in_dim.26), calls=%async_computation | async-start | bytes 8192 | tf_op jit(solution)/shard_map/all_to_all | solution.py:44
  13.7 30.1 %all-to-all-start.2 = ((bf16[128,8,512]{2,0,1:T(8,128)(2,1)}), bf16[128,8,512]{2,0,1:T(8,128)(2,1)S(1)}, u32[]{:S(2)}, u32[]{:S(2)}) async-start(bf16[128,8,512]{2,0,1:T(8,128)(2,1)} %copy.30), calls=%async_computation.2 | async-start | bytes 2097152 | tf_op jit(solution)/shard_map/all_to_all | solution.py:43
  43.8 8.4 %all-to-all-start.1 = ((s32[4,256,1]{1,2,0:T(1,128)}), s32[4,256,1]{1,2,0:T(1,128)S(1)}, u32[]{:S(2)}, u32[]{:S(2)}) async-start(s32[4,256,1]{1,2,0:T(1,128)} %copy.26), calls=%async_computation.1 | async-start | bytes 8192 | tf_op jit(solution)/shard_map/all_to_all | solution.py:51
  52.2 15.7 %all-to-all-start.3 = ((bf16[4,256,512]{2,1,0:T(8,128)(2,1)}), bf16[4,256,512]{2,1,0:T(8,128)(2,1)S(1)}, u32[]{:S(2)}, u32[]{:S(2)}) async-start(bf16[4,256,512]{2,1,0:T(8,128)(2,1)} %bitcast.10), calls=%async_computation.3 | async-start | bytes 2097152 | tf_op jit(solution)/shard_map/all_to_all | solution.py:50
where the time goes:
time: 93.3 us; the launch traced here: 92.9 us
  waiting for transfers between devices  41.9 us (45%)
  matrix products  21.2 us (23%)
  starting transfers between devices  17.1 us (18%)
  local copies, waits for them, and re-layouts  6.29 us (7%)
  other arithmetic  5.63 us (6%)
    all_to_all x1, waiting for transfers between devices, local(): lax.all_to_all(grads, 'dp', split_axis=1, concat_axis=0, tiled=True)  24.1 us
    dot_general x2, matrix products, accumulate(): lax.dot_general(onehot.astype(block.dtype), block, (((0,), (0,)), ((), ()...  20.7 us
    all_to_all x1, waiting for transfers between devices, local(): lax.all_to_all(rows, 'vocab', split_axis=0, concat_axis=0, tiled=True)  12.1 us
    all_to_all x1, starting transfers between devices, local(): lax.all_to_all(spread_ids, 'dp', split_axis=1, concat_axis=0, tiled=True)  6.35 us
    all_to_all x1, starting transfers between devices, local(): lax.all_to_all(slot_ids, 'vocab', split_axis=0, concat_axis=0, tiled=True)  3.72 us
    reduce_sum x2, other arithmetic, accumulate(): counts = counts + jnp.sum(onehot.astype(jnp.float32), axis=0)  3.68 us
    all_to_all x1, starting transfers between devices, local(): lax.all_to_all(grads, 'dp', split_axis=1, concat_axis=0, tiled=True)  3.56 us
    all_to_all x1, starting transfers between devices, local(): lax.all_to_all(rows, 'vocab', split_axis=0, concat_axis=0, tiled=True)  3.52 us
  transfers between devices with their start and end apart: 4, of which 4 were waited for; matrix products, arithmetic and copies ran while one was open for 7% of the time, Pallas kernels for 0%

commit v1 on v0

--- a/solution.py
+++ b/solution.py
@@ -1,3 +1,4 @@
+import functools
 import math
 import jax
 import jax.numpy as jnp
@@ -7,6 +8,21 @@
 VOCAB_DEV = 8016
 TOK_DEV = 128
 CAP = 32
+
+
+def match_plane(s0, dim_i, axis_k):
+    return jnp.concatenate(
+        lax.all_to_all(
+            jnp.stack(jnp.split(s0, lax.axis_size("dp"), axis=axis_k), axis=0),
+            axis_name="dp",
+            split_axis=0,
+            concat_axis=0,
+        ),
+        axis=dim_i,
+    )
+
+
+members_all_measure = functools.partial(match_plane, dim_i=0, axis_k=1)
 
 
 def bucket(id_blocks, data_blocks, n_vocab):
@@ -41,7 +57,7 @@
     spread_ids = jnp.broadcast_to(token_ids[:, None], (token_ids.shape[0], n_data))
     split_rows, split_ids = (
         lax.all_to_all(grads, "dp", split_axis=1, concat_axis=0, tiled=True),
-        lax.all_to_all(spread_ids, "dp", split_axis=1, concat_axis=0, tiled=True),
+        members_all_measure(spread_ids),
     )
     group_ids = split_ids.reshape(n_data, -1)
     group_rows = split_rows.reshape(n_data, group_ids.shape[1], split_rows.shape[1])

time: 93.3 us -> 93.3 us (level)
    another operation x0 -> x1, local copies, waits for them, and re-layouts: none -> 1.25 us  [match_plane(): jnp.stack(jnp.split(s0, lax.axis_size('dp'), axis=axis_k), axis=0)]
    broadcast_in_dim x1 -> x0, local copies, waits for them, and re-layouts: 1.25 us -> none  [local(): jnp.broadcast_to(token_ids[:, None], (token_ids.shape[0], n_data))]
where the time goes in v1:
time: 93.3 us; the launch traced here: 92.9 us
  waiting for transfers between devices  41.9 us (45%)
  matrix products  21.2 us (23%)
  starting transfers between devices  17.1 us (18%)
  local copies, waits for them, and re-layouts  6.29 us (7%)
  other arithmetic  5.63 us (6%)
    all_to_all x1, waiting for transfers between devices, local(): lax.all_to_all(grads, 'dp', split_axis=1, concat_axis=0, tiled=True)  24.1 us
    dot_general x2, matrix products, accumulate(): lax.dot_general(onehot.astype(block.dtype), block, (((0,), (0,)), ((), ()...  20.7 us
    all_to_all x1, waiting for transfers between devices, local(): lax.all_to_all(rows, 'vocab', split_axis=0, concat_axis=0, tiled=True)  12.1 us
    all_to_all x1, starting transfers between devices, match_plane(): lax.all_to_all(jnp.stack(jnp.split(s0, lax.axis_size('dp'), axis=axis_k),...  6.35 us
    all_to_all x1, starting transfers between devices, local(): lax.all_to_all(slot_ids, 'vocab', split_axis=0, concat_axis=0, tiled=True)  3.72 us
    reduce_sum x2, other arithmetic, accumulate(): counts = counts + jnp.sum(onehot.astype(jnp.float32), axis=0)  3.68 us
    all_to_all x1, starting transfers between devices, local(): lax.all_to_all(grads, 'dp', split_axis=1, concat_axis=0, tiled=True)  3.56 us
    all_to_all x1, starting transfers between devices, local(): lax.all_to_all(rows, 'vocab', split_axis=0, concat_axis=0, tiled=True)  3.52 us
  transfers between devices with their start and end apart: 4, of which 4 were waited for; matrix products, arithmetic and copies ran while one was open for 7% of the time, Pallas kernels for 0%

profile of v1, /device:TPU:0, one launch (start us, length us, event | category | flops | bytes accessed | tf_op | source)
XLA Modules:
  0.0 92.9 jit_solution(14292049239312270715)
XLA Ops:
  0.6 1.3 %stack.2 = s32[8,128,1]{1,2,0:T(1,128)} broadcast(s32[128]{0:T(128)} %param.5), dimensions={1} | broadcast | bytes 4608 | tf_op jit(solution)/shard_map/stack | solution.py:16
  1.9 6.4 %all-to-all-start = ((s32[8,128,1]{1,2,0:T(1,128)}), s32[8,128,1]{1,2,0:T(1,128)S(1)}, u32[]{:S(2)}, u32[]{:S(2)}) async-start(s32[8,128,1]{1,2,0:T(1,128)} %stack.2), calls=%async_computation | async-start | bytes 8192 | tf_op jit(solution)/shard_map/all_to_all | solution.py:15
  8.2 1.6 %copy.29 = bf16[128,4096]{0,1:T(8,128)(2,1)S(1)} copy(bf16[128,4096]{1,0:T(8,128)(2,1)} %param.4) | data formatting | bytes 2097152 | tf_op args[0]
  9.9 1.3 %copy.30 = bf16[128,8,512]{2,0,1:T(8,128)(2,1)} copy(bf16[128,8,512]{0,2,1:T(8,128)(2,1)S(1)} %bitcast.27) | data formatting | bytes 2097152 | tf_op jit(solution)/shard_map/all_to_all | solution.py:59
  11.2 2.6 %all-to-all-done = s32[8,128,1]{1,2,0:T(1,128)S(1)} async-done(((s32[8,128,1]{1,2,0:T(1,128)}), s32[8,128,1]{1,2,0:T(1,128)S(1)}, u32[]{:S(2)}, u32[]{:S(2)}) %all-to-all-start) | async-done | bytes 4128 | tf_op jit(solution)/shard_map/all_to_all | solution.py:15
  13.7 3.6 %all-to-all-start.2 = ((bf16[128,8,512]{2,0,1:T(8,128)(2,1)}), bf16[128,8,512]{2,0,1:T(8,128)(2,1)S(1)}, u32[]{:S(2)}, u32[]{:S(2)}) async-start(bf16[128,8,512]{2,0,1:T(8,128)(2,1)} %copy.30), calls=%async_computation.2 | async-start | bytes 2097152 | tf_op jit(solution)/shard_map/all_to_all | solution.py:59
  17.3 0.1 add.37
  17.4 0.2 convert_reduce_fusion
  17.6 0.1 iota_compare_fusion.5
  17.7 0.1 copy.23
  17.8 0.1 iota_add_fusion
  17.9 0.9 select_reduce_fusion
  18.8 0.1 reduce_sum.31
  18.9 0.1 lt.57
  19.0 0.1 lt.58
  19.1 0.6 copy.26
  19.7 24.1 %all-to-all-done.2 = bf16[128,8,512]{2,0,1:T(8,128)(2,1)S(1)} async-done(((bf16[128,8,512]{2,0,1:T(8,128)(2,1)}), bf16[128,8,512]{2,0,1:T(8,128)(2,1)S(1)}, u32[]{:S(2)}, u32[]{:S(2)}) %all-to-all-start.2) | async-done | bytes 1048608 | tf_op jit(solution)/shard_map/all_to_all | solution.py:59
  43.8 3.7 %all-to-all-start.1 = ((s32[4,256,1]{1,2,0:T(1,128)}), s32[4,256,1]{1,2,0:T(1,128)S(1)}, u32[]{:S(2)}, u32[]{:S(2)}) async-start(s32[4,256,1]{1,2,0:T(1,128)} %copy.26), calls=%async_computation.1 | async-start | bytes 8192 | tf_op jit(solution)/shard_map/all_to_all | solution.py:67
  47.5 0.5 fusion.9
  48.0 1.1 %copy.31 = bf16[4,8,32,512]{3,2,1,0:T(8,128)(2,1)} copy(bf16[4,8,32,512]{3,2,0,1:T(8,128)(2,1)S(1)} %fusion.9) | data formatting | bytes 2097152 | tf_op jit(solution)/shard_map/convert_element_type | solution.py:48
  49.1 3.1 %all-to-all-done.1 = s32[4,256,1]{1,2,0:T(1,128)S(1)} async-done(((s32[4,256,1]{1,2,0:T(1,128)}), s32[4,256,1]{1,2,0:T(1,128)S(1)}, u32[]{:S(2)}, u32[]{:S(2)}) %all-to-all-start.1) | async-done | bytes 4128 | tf_op jit(solution)/shard_map/all_to_all | solution.py:67
  52.2 3.5 %all-to-all-start.3 = ((bf16[4,256,512]{2,1,0:T(8,128)(2,1)}), bf16[4,256,512]{2,1,0:T(8,128)(2,1)S(1)}, u32[]{:S(2)}, u32[]{:S(2)}) async-start(bf16[4,256,512]{2,1,0:T(8,128)(2,1)} %bitcast.8), calls=%async_computation.3 | async-start | bytes 2097152 | tf_op jit(solution)/shard_map/all_to_all | solution.py:66
  55.8 12.1 %all-to-all-done.3 = bf16[4,256,512]{2,1,0:T(8,128)(2,1)S(1)} async-done(((bf16[4,256,512]{2,1,0:T(8,128)(2,1)}), bf16[4,256,512]{2,1,0:T(8,128)(2,1)S(1)}, u32[]{:S(2)}, u32[]{:S(2)}) %all-to-all-start.3) | async-done | bytes 1048608 | tf_op jit(solution)/shard_map/all_to_all | solution.py:66
  67.9 24.4 %while.13 = (s32[]{:T(128)}, f32[8016,512]{1,0:T(8,128)}, f32[8016]{0:T(1024)S(1)}, s32[2,512]{1,0:T(2,128)S(1)}, bf16[2,512,512]{2,1,0:T(8,128)(2,1)S(1)}, /*index=5*/s32[]{:T(128)}, s32[]{:T(128)}) while((s32[]{:T(128)}, f32[8016,512]{1,0:T(8,128)}, f32[8016]{0:T(1024)S(1)}, s32[2,512]{1,0:T(2,128)S(1)}, ...), condition=%wide.region_4.5_spmd.clone, body=%wide.region_2.4_spmd.clone.sunk | while | flops 4227325952 | bytes 33494372 | solution.py:93
  67.9 1.8 %fusion.18 = f32[8016]{0:T(1024)S(1)} fusion(s32[512]{0:T(512)S(1)} %bitcast.28), kind=kLoop, calls=%fused_computation.4.clone.1 | loop fusion | flops 12304560 | bytes 34112 | tf_op jit(solution)/shard_map/while/body/eval_jaxpr/reduce_sum | solution.py:86
  69.7 8.7 %select_add_fusion.4 = f32[8016,512]{1,0:T(8,128)} fusion(f32[8016,512]{1,0:T(8,128)} %get-tuple-element.106, s32[512]{0:T(512)S(1)} %bitcast.29, pred[]{:T(512)S(6)} %compare.4, bf16[2,512,512]{2,1,0:T(8,128)(2,1)S(1)} %get-tuple-element.116, s32[]{:T(128)S(6)} %copy.37), kind=kOutput, calls=%fused_computation.5.clone.1 | convolution fusion | flops 4215005184 | bytes 33359876 | tf_op jit(solution)/shard_map/while/body/eval_jaxpr/dot_general | solution.py:80
  78.4 1.8 %fusion.18 = f32[8016]{0:T(1024)S(1)} fusion(s32[512]{0:T(512)S(1)} %bitcast.28), kind=kLoop, calls=%fused_computation.4.clone.1 | loop fusion | flops 12304560 | bytes 34112 | tf_op jit(solution)/shard_map/while/body/eval_jaxpr/reduce_sum | solution.py:86
  80.3 12.0 %select_add_fusion.4 = f32[8016,512]{1,0:T(8,128)} fusion(f32[8016,512]{1,0:T(8,128)} %get-tuple-element.106, s32[512]{0:T(512)S(1)} %bitcast.29, pred[]{:T(512)S(6)} %compare.4, bf16[2,512,512]{2,1,0:T(8,128)(2,1)S(1)} %get-tuple-element.116, s32[]{:T(128)S(6)} %copy.37), kind=kOutput, calls=%fused_computation.5.clone.1 | convolution fusion | flops 4215005184 | bytes 33359876 | tf_op jit(solution)/shard_map/while/body/eval_jaxpr/dot_general | solution.py:80
  92.3 0.6 broadcast_multiply_fusion
  (15 shorter events, 0.1 us)
Async XLA Ops:
  1.9 11.9 %all-to-all-start = ((s32[8,128,1]{1,2,0:T(1,128)}), s32[8,128,1]{1,2,0:T(1,128)S(1)}, u32[]{:S(2)}, u32[]{:S(2)}) async-start(s32[8,128,1]{1,2,0:T(1,128)} %stack.2), calls=%async_computation | async-start | bytes 8192 | tf_op jit(solution)/shard_map/all_to_all | solution.py:15
  13.7 30.1 %all-to-all-start.2 = ((bf16[128,8,512]{2,0,1:T(8,128)(2,1)}), bf16[128,8,512]{2,0,1:T(8,128)(2,1)S(1)}, u32[]{:S(2)}, u32[]{:S(2)}) async-start(bf16[128,8,512]{2,0,1:T(8,128)(2,1)} %copy.30), calls=%async_computation.2 | async-start | bytes 2097152 | tf_op jit(solution)/shard_map/all_to_all | solution.py:59
  43.8 8.4 %all-to-all-start.1 = ((s32[4,256,1]{1,2,0:T(1,128)}), s32[4,256,1]{1,2,0:T(1,128)S(1)}, u32[]{:S(2)}, u32[]{:S(2)}) async-start(s32[4,256,1]{1,2,0:T(1,128)} %copy.26), calls=%async_computation.1 | async-start | bytes 8192 | tf_op jit(solution)/shard_map/all_to_all | solution.py:67
  52.2 15.7 %all-to-all-start.3 = ((bf16[4,256,512]{2,1,0:T(8,128)(2,1)}), bf16[4,256,512]{2,1,0:T(8,128)(2,1)S(1)}, u32[]{:S(2)}, u32[]{:S(2)}) async-start(bf16[4,256,512]{2,1,0:T(8,128)(2,1)} %bitcast.8), calls=%async_computation.3 | async-start | bytes 2097152 | tf_op jit(solution)/shard_map/all_to_all | solution.py:66
